TPU v7x, 32 devices: a whole 2x2x4 slice. The times are simulated.
32 devices in a mesh: grp: 2 (over x), tm: 16 (over z, y, core).
Axes of the slice: x: 2, y: 2, z: 4, core: 2. Of those that a mesh axis runs over, the one named last changes fastest.
Arguments:
- samples: bfloat16 [16, 2097152], P('grp', 'tm'), parts along dimension 0, may hold values from -128 to 127, as said below
- filter_taps: bfloat16 [16, 8192], replicated, may hold values from -4 to 4
Outputs:
- channelized: bfloat16 [16, 2, 4096, 256], P('grp', None, 'tm'), parts along dimension 0
There are 2 independent parts, one for each index of `grp`. A program takes and returns all parts, laid end to end along the dimension named above; an argument that names none is the same for every part. Nothing has to cross between parts.
Inputs may be any that keep to these rules, and one draw needn't show every extreme that they name: `samples`: every sample is a whole number, as from an 8-bit converter.
All inputs are finite; a program needn't handle non-finite values.
Results may differ from a plain program's by a relative error of at most 0.007.
Values may be sent and summed in bfloat16 or wider, within the bound.
A program may use at most 128 MiB of HBM per device.

v0:
```python
import jax
import jax.numpy as jnp
from jax import lax
from jax.sharding import PartitionSpec as P

ROW_LEN = 128


target_level = 0.378
epsilon = 1e-06


def shifted(value, axis, by):
    size = lax.axis_size(axis)
    pairs = [(i, i + by) for i in range(size) if 0 <= i + by < size]
    return lax.ppermute(value, axis, pairs)


def tables(row_len, col_len):
    fft_len = row_len * col_len
    rows_a = jnp.arange(row_len, dtype=jnp.int32)
    cols_b = jnp.arange(col_len, dtype=jnp.int32)
    half_c = jnp.arange(col_len // 2, dtype=jnp.int32)
    angle_a = (
        2.0 * jnp.pi / row_len * (rows_a[:, None] * rows_a[None, :] % row_len).astype(jnp.float32)
    )
    angle_t = (
        2.0 * jnp.pi / fft_len * (cols_b[:, None] * rows_a[None, :] % fft_len).astype(jnp.float32)
    )
    angle_b = (
        2.0 * jnp.pi / col_len * (cols_b[:, None] * half_c[None, :] % col_len).astype(jnp.float32)
    )
    return (
        jnp.cos(angle_a).astype(jnp.bfloat16),
        jnp.sin(angle_a).astype(jnp.bfloat16),
        jnp.cos(angle_t),
        jnp.sin(angle_t),
        jnp.cos(angle_b).astype(jnp.bfloat16),
        jnp.sin(angle_b).astype(jnp.bfloat16),
    )


def transform(filtered):
    streams, frames, fft_len = filtered.shape
    col_len = fft_len // ROW_LEN
    cos_a, sin_a, cos_t, sin_t, cos_b, sin_b = tables(ROW_LEN, col_len)
    blocks = filtered.reshape(streams, frames, ROW_LEN, col_len)
    first_re = jnp.einsum("sfab,ad->sfbd", blocks, cos_a, preferred_element_type=jnp.float32)
    first_im = -jnp.einsum("sfab,ad->sfbd", blocks, sin_a, preferred_element_type=jnp.float32)
    twisted_re = (first_re * cos_t + first_im * sin_t).astype(jnp.bfloat16)
    twisted_im = (first_im * cos_t - first_re * sin_t).astype(jnp.bfloat16)
    spec_re = jnp.einsum(
        "sfbd,bc->scdf", twisted_re, cos_b, preferred_element_type=jnp.float32
    ) + jnp.einsum("sfbd,bc->scdf", twisted_im, sin_b, preferred_element_type=jnp.float32)
    spec_im = jnp.einsum(
        "sfbd,bc->scdf", twisted_im, cos_b, preferred_element_type=jnp.float32
    ) - jnp.einsum("sfbd,bc->scdf", twisted_re, sin_b, preferred_element_type=jnp.float32)
    return (spec_re.reshape(streams, -1, frames), spec_im.reshape(streams, -1, frames))


def on_device(samples, filter_taps):
    streams = samples.shape[0]
    tap_count, fft_len = filter_taps.shape
    frames = samples.shape[1] // fft_len
    signal = samples.reshape(streams, frames, fft_len)
    history = shifted(signal[:, frames - (tap_count - 1) :, :], "tm", 1)
    extended = jnp.concatenate([history, signal], axis=1)
    weights = filter_taps.astype(jnp.float32)
    filtered = jnp.zeros((streams, frames, fft_len), jnp.float32)
    for tap_index in range(tap_count):
        offset = tap_count - 1 - tap_index
        filtered = filtered + weights[tap_index] * extended[:, offset : offset + frames].astype(
            jnp.float32
        )
    filtered = filtered.astype(jnp.bfloat16)
    spec_re, spec_im = transform(filtered)
    real_part = spec_re.astype(jnp.bfloat16)
    imag_part = spec_im.astype(jnp.bfloat16)
    real_wide = real_part.astype(jnp.float32)
    imag_wide = imag_part.astype(jnp.float32)
    local_power = jnp.sum(real_wide * real_wide + imag_wide * imag_wide, axis=(1, 2))
    total_power = lax.psum(local_power, "tm")
    count = frames * lax.axis_size("tm") * spec_re.shape[1]
    gain = target_level / jnp.sqrt(total_power / count + epsilon)
    scaled = jnp.stack(
        [
            jnp.clip(real_wide * gain[:, None, None], -1.0, 1.0),
            jnp.clip(imag_wide * gain[:, None, None], -1.0, 1.0),
        ],
        axis=1,
    ).astype(jnp.bfloat16)
    result = lax.all_to_all(scaled, "tm", split_axis=2, concat_axis=3, tiled=True)
    return result


def solution(mesh):
    return jax.shard_map(
        on_device,
        mesh=mesh,
        in_specs=(P("grp", "tm"), P()),
        out_specs=P("grp", None, "tm", None),
        check_vma=False,
    )
```

profile of v0, /device:TPU:0, one launch (start us, length us, event | category | flops | bytes accessed | tf_op | source)
XLA Modules:
  0.0 244.0 jit_solution(3988610349749079119)
XLA Ops:
  0.0 1.8 slice.130
  1.8 2.5 %collective-permute-start = (bf16[8,15,8192]{2,0,1:T(8,128)(2,1)S(1)}, bf16[8,15,8192]{2,0,1:T(8,128)(2,1)S(1)}, u32[]{:S(2)}, u32[]{:S(2)}) collective-permute-start(bf16[8,15,8192]{2,0,1:T(8,128)(2,1)S(1)} %slice.130), channel_id=1, source_target_pairs={{0,1},{1,2},{2,3},{3,4},{4,5},{5,6},{6,7},{7,8},{8,9},{9,10},{10,1... | collective-permute-start | bytes 5898248 | tf_op jit(solution)/shard_map/ppermute | solution.py:16
  5.0 2.8 %collective-permute-done = bf16[8,15,8192]{2,0,1:T(8,128)(2,1)S(1)} collective-permute-done((bf16[8,15,8192]{2,0,1:T(8,128)(2,1)S(1)}, bf16[8,15,8192]{2,0,1:T(8,128)(2,1)S(1)}, u32[]{:S(2)}, u32[]{:S(2)}) %collective-permute-start) | collective-permute-done | bytes 1966112 | tf_op jit(solution)/shard_map/ppermute | solution.py:16
  7.8 8.7 %add_convert_fusion.1 = bf16[8,16,8192]{2,0,1:T(8,128)(2,1)S(1)} fusion(bf16[8,16,8192]{2,0,1:T(8,128)(2,1)S(1)} %bitcast.84, bf16[8,15,8192]{2,0,1:T(8,128)(2,1)S(1)} %collective-permute-done, f32[8192]{0:T(1024)S(1)} %bitcast.100, f32[8192]{0:T(1024)S(1)} %bitcast.99, f32[8192]{0:T(1024)S(1)} %bitcast.98, f32[8192]{0:T(1024)S(1)} %bitcast.97, ...), kind=kLoop, calls=%fused_computation.30 | loop fusion | flops 66060288 | bytes 6684672 | tf_op jit(solution)/shard_map/convert_element_type | solution.py:75
  16.5 1.2 copy.27
  17.7 5.5 %reshape.106 = bf16[8,16,128,64]{3,2,1,0:T(8,128)(2,1)} reshape(bf16[8,16,8192]{2,1,0:T(8,128)(2,1)S(1)} %copy.27) | data formatting | bytes 4194304 | tf_op jit(solution)/shard_map/reshape | solution.py:47
  23.2 3.7 %fusion.33 = f32[8,16,64,128]{3,2,1,0:T(8,128)S(1)} fusion(bf16[8,16,128,64]{3,2,1,0:T(8,128)(2,1)} %reshape.106), kind=kOutput, calls=%fused_computation.81 | convolution fusion | flops 268681216 | bytes 6291456 | tf_op jit(solution)/shard_map/sfab,ad->sfbd/dot_general | solution.py:49
  26.9 1.7 add_convert_fusion
  28.7 0.5 fusion.54
  29.2 0.5 fusion.52
  29.7 0.5 add_convert_fusion.2
  30.2 1.6 convert_bitcast_fusion
  31.8 0.8 fusion.1
  32.6 50.9 %psum.7 = f32[8]{0:T(128)S(1)} all-reduce(f32[8]{0:T(128)S(1)} %get-tuple-element.25), channel_id=1, replica_groups=mesh['grp'=2,'tm'=16] {'tm'}, use_global_device_ids=true, to_apply=%region_1.2 | all-reduce | flops 8 | bytes 64 | tf_op jit(solution)/shard_map/psum | solution.py:82
  83.5 1.8 reshape.107
  85.3 1.6 convert_bitcast_fusion.1
  86.9 2.7 %reshape.108 = f32[8,1,4096,16]{2,3,0,1:T(8,128)} reshape(f32[8,32,128,16]{2,1,3,0:T(8,128)} %convert_bitcast_fusion.1) | data formatting | bytes 4194304 | tf_op jit(solution)/shard_map/convert_element_type | solution.py:80
  89.6 2.0 fusion.19
  91.9 27.8 %copy.32 = bf16[8,2,4096,16]{3,1,0,2:T(2,128)(2,1)} copy(bf16[8,2,4096,16]{2,3,1,0:T(8,128)(2,1)S(1)} %pad_maximum_fusion.1) | data formatting | bytes 4194304 | tf_op jit(solution)/shard_map/stack | solution.py:85
  119.7 19.7 %reshape.113 = bf16[16,2,32768]{2,1,0:T(2,128)(2,1)S(1)} reshape(bf16[4096,8,2,16]{3,2,1,0:T(2,128)(2,1)} %bitcast.80) | data formatting | bytes 4194304
  139.4 50.5 %all_to_all.18 = bf16[16,2,32768]{2,1,0:T(2,128)(2,1)} all-to-all(bf16[16,2,32768]{2,1,0:T(2,128)(2,1)S(1)} %reshape.113), channel_id=1, replica_groups=mesh['grp'=2,'tm'=16] {'tm'}, dimensions={0} | all-to-all | bytes 4194304 | tf_op jit(solution)/shard_map/all_to_all | solution.py:92
  189.9 16.5 %reshape.114 = bf16[4096,8,2,16]{3,2,1,0:T(2,128)(2,1)} reshape(bf16[16,2,32768]{2,1,0:T(2,128)(2,1)} %all_to_all.18) | data formatting | bytes 4194304
  206.4 35.3 %copy.43 = bf16[8,2,16,256,16]{3,4,2,1,0:T(8,128)(2,1)S(1)} copy(bf16[8,2,16,256,16]{4,1,0,3,2:T(2,128)(2,1)} %bitcast.81) | data formatting | bytes 4194304 | tf_op jit(solution)/shard_map/all_to_all | solution.py:92
  241.6 2.4 copy.35
  (10 shorter events, 0.8 us)
Async XLA Ops:
  0.0 4.5 %copy-start.2 = (bf16[16,8192]{1,0:T(8,128)(2,1)S(1)}, bf16[16,8192]{1,0:T(8,128)(2,1)}, u32[]{:S(2)}) copy-start(bf16[16,8192]{1,0:T(8,128)(2,1)} %param.3) | copy-start | bytes 786436
  0.0 7.8 %copy-start.1 = (bf16[8,131072]{1,0:T(8,128)(2,1)S(1)}, bf16[8,131072]{1,0:T(8,128)(2,1)}, u32[]{:S(2)}) copy-start(bf16[8,131072]{1,0:T(8,128)(2,1)} %param.2) | copy-start | bytes 6291460
  1.8 6.0 %collective-permute-start = (bf16[8,15,8192]{2,0,1:T(8,128)(2,1)S(1)}, bf16[8,15,8192]{2,0,1:T(8,128)(2,1)S(1)}, u32[]{:S(2)}, u32[]{:S(2)}) collective-permute-start(bf16[8,15,8192]{2,0,1:T(8,128)(2,1)S(1)} %slice.130), channel_id=1, source_target_pairs={{0,1},{1,2},{2,3},{3,4},{4,5},{5,6},{6,7},{7,8},{8,9},{9,10},{10,1... | collective-permute-start | bytes 5898248 | tf_op jit(solution)/shard_map/ppermute | solution.py:16
  23.2 3.7 %copy-start = (bf16[8,16,128,64]{3,2,1,0:T(8,128)(2,1)S(1)}, bf16[8,16,128,64]{3,2,1,0:T(8,128)(2,1)}, u32[]{:S(2)}) copy-start(bf16[8,16,128,64]{3,2,1,0:T(8,128)(2,1)} %reshape.106) | copy-start | bytes 6291460
where the time goes:
time: 246 us; the launch traced here: 244 us
  local copies, waits for them, and re-layouts  115 us (47%)
  blocking collectives  101 us (41%)
  other arithmetic  14.3 us (6%)
  matrix products  7.76 us (3%)
  waiting for transfers between devices  2.82 us (1%)
  starting transfers between devices  2.52 us (1%)
    psum x1, blocking collectives, on_device(): total_power = lax.psum(local_power, 'tm')  50.9 us
    all_to_all x1, blocking collectives, on_device(): lax.all_to_all(scaled, 'tm', split_axis=2, concat_axis=3, tiled=True)  50.5 us
    all_to_all x2, local copies, waits for them, and re-layouts, on_device(): lax.all_to_all(scaled, 'tm', split_axis=2, concat_axis=3, tiled=True)  37.7 us
    unnamed x8, local copies, waits for them, and re-layouts  36.2 us
    another operation x1, local copies, waits for them, and re-layouts, on_device(): jnp.stack([jnp.clip(real_wide * gain[:, None, None], -1.0, 1.0), jnp.clip...  27.8 us
    convert_element_type x1, other arithmetic, on_device(): filtered = filtered.astype(jnp.bfloat16)  8.7 us
    reshape x1, local copies, waits for them, and re-layouts, transform(): blocks = filtered.reshape(streams, frames, ROW_LEN, col_len)  5.54 us
  transfers between devices with their start and end apart: 1, of which 1 were waited for; matrix products, arithmetic and copies ran while one was open for 0% of the time, Pallas kernels for 0%

commit v1 on v0

--- a/solution.py
+++ b/solution.py
@@ -1,9 +1,276 @@
+import functools
+
 import jax
 import jax.numpy as jnp
+import numpy as np
 from jax import lax
+from jax.experimental import pallas as pl
+from jax.experimental.pallas import tpu as pltpu
 from jax.sharding import PartitionSpec as P
 
 ROW_LEN = 128
+LANES = 128
+MESH = pl.DeviceIdType.MESH
+
+
+def kernel_tables(row_len, col_len):
+    fft_len = row_len * col_len
+    a = np.arange(row_len)
+    b = np.arange(col_len)
+    c = np.arange(col_len // 2)
+    pi2 = 2.0 * np.pi
+    order = np.concatenate([a[0::2], a[1::2]])
+    angle_a = (np.float32(pi2 / row_len) * (a[:, None] * order[None, :] % row_len).astype(np.float32)).astype(np.float64)
+    stage_a = np.concatenate([np.cos(angle_a), -np.sin(angle_a)], axis=0)
+    angle_t = (np.float32(pi2 / fft_len) * (a[:, None] * b[None, :] % fft_len).astype(np.float32)).astype(np.float64)
+    cos_t = np.tile(np.cos(angle_t), (1, 2))
+    sin_t = np.tile(np.sin(angle_t), (1, 2))
+    angle_b = (np.float32(pi2 / col_len) * (c[:, None] * b[None, :] % col_len).astype(np.float32)).astype(np.float64)
+    cos_b, sin_b = np.cos(angle_b), np.sin(angle_b)
+    rows = 2 * len(c)
+    stage_b = np.zeros((2 * rows, 4 * col_len))
+    re_part = np.concatenate([cos_b, -sin_b], axis=0)
+    im_part = np.concatenate([sin_b, cos_b], axis=0)
+    for f in range(2):
+        at = slice(f * rows, (f + 1) * rows)
+        stage_b[at, f * col_len : (f + 1) * col_len] = re_part
+        stage_b[at, (2 + f) * col_len : (3 + f) * col_len] = im_part
+    return (
+        jnp.asarray(stage_a, jnp.bfloat16),
+        jnp.asarray(cos_t, jnp.float32),
+        jnp.asarray(sin_t, jnp.float32),
+        jnp.asarray(stage_b, jnp.bfloat16),
+    )
+
+
+def body(
+    n, count, x_ref, taps_ref, ta_ref, ct_ref, st_ref, tb_ref, eye_ref, out_ref,
+    xf, wf, ext, ybuf, gbuf, spec, recv, pbuf, pall, gain_buf,
+    halo_send, halo_recv, spec_send, spec_recv, own_sem, pow_send, pow_recv, pow_own,
+):
+    me = lax.axis_index("tm")
+    streams = x_ref.shape[0]
+    taps, fft_len = taps_ref.shape
+    hist = taps - 1
+    frames = x_ref.shape[1] // fft_len
+    rows = fft_len // LANES
+    rc = gbuf.shape[0] // frames
+    half_c = rc // 2
+    ch = out_ref.shape[2]
+    cb = ch // LANES
+
+    barrier = pltpu.get_barrier_semaphore()
+
+    @pl.loop(1, n)
+    def _(o):
+        pl.semaphore_signal(barrier, inc=1, device_id={"tm": lax.rem(me + o, n)}, device_id_type=MESH)
+
+    unroll = 16
+
+    @pl.loop(0, frames * rows // unroll)
+    def _(i):
+        for u in range(unroll):
+            q = i * unroll + u
+            v = x_ref[:, pl.ds(pl.multiple_of(q * LANES, LANES), LANES)].astype(jnp.float32)
+            xf[pl.ds(q, streams, stride=frames * rows), :] = v
+
+    @pl.loop(0, streams)
+    def _(s):
+        @pl.loop(0, frames)
+        def _(f):
+            at = pl.multiple_of((s * frames + f) * rows, rows)
+            ext[s, hist + f] = xf[pl.ds(at, rows), :].astype(jnp.bfloat16)
+
+    pl.semaphore_wait(barrier, n - 1)
+
+    def halo_copy(s):
+        return pltpu.make_async_remote_copy(
+            src_ref=ext.at[s, pl.ds(frames, hist)],
+            dst_ref=ext.at[s, pl.ds(0, hist)],
+            send_sem=halo_send.at[s],
+            recv_sem=halo_recv.at[s],
+            device_id={"tm": lax.rem(me + 1, n)},
+            device_id_type=MESH,
+        )
+
+    @pl.when(me < n - 1)
+    def _():
+        @pl.loop(0, streams)
+        def _(s):
+            halo_copy(s).start()
+
+    @pl.when(me == 0)
+    def _():
+        @pl.loop(0, streams)
+        def _(s):
+            ext[s, pl.ds(0, hist)] = jnp.zeros((hist, rows, LANES), jnp.bfloat16)
+
+    @pl.loop(0, rows)
+    def _(r):
+        w = taps_ref[:, pl.ds(pl.multiple_of(r * LANES, LANES), LANES)].astype(jnp.float32)
+        wf[pl.ds(r, taps, stride=rows), :] = w
+
+    low = lax.broadcasted_iota(jnp.int32, (16, LANES), 1) < LANES // 2
+
+    @pl.loop(0, streams)
+    def _(s):
+        @pl.when(me > 0)
+        def _():
+            halo_copy(s).wait_recv()
+
+        @pl.loop(0, rows // 16)
+        def _(rb):
+            r0 = pl.multiple_of(rb * 16, 16)
+            acc = [None] * frames
+            w = [wf[pl.ds(p * rows + r0, 16), :] for p in range(taps)]
+            for i in range(hist + frames - 1, -1, -1):
+                xi = ext[s, i, pl.ds(r0, 16), :].astype(jnp.float32)
+                for f in range(frames):
+                    p = f + hist - i
+                    if 0 <= p < taps:
+                        term = w[p] * xi
+                        acc[f] = term if acc[f] is None else acc[f] + term
+            for q in range(frames // 2):
+                f0, f1 = acc[2 * q], acc[2 * q + 1]
+                y0 = jnp.where(low, f0, pltpu.roll(f1, LANES // 2, 1))
+                y1 = jnp.where(low, pltpu.roll(f0, LANES // 2, 1), f1)
+                ybuf[q, pl.ds(r0, 16), :] = y0.astype(jnp.bfloat16)
+                ybuf[q, pl.ds(rows + r0, 16), :] = y1.astype(jnp.bfloat16)
+
+        @pl.loop(0, frames // 4)
+        def _(g):
+            y = jnp.concatenate([ybuf[2 * g], ybuf[2 * g + 1]], axis=1)
+            first = jnp.dot(ta_ref[...], y, preferred_element_type=jnp.float32)
+            for u in range(2):
+                re = first[:ROW_LEN, u * LANES : (u + 1) * LANES]
+                im = first[ROW_LEN:, u * LANES : (u + 1) * LANES]
+                ct, st = ct_ref[...], st_ref[...]
+                tw = jnp.concatenate(
+                    [(re * ct + im * st).astype(jnp.bfloat16), (im * ct - re * st).astype(jnp.bfloat16)],
+                    axis=1,
+                )
+                sp = lax.dot_general(
+                    tb_ref[...], tw, (((1,), (1,)), ((), ())), preferred_element_type=jnp.float32
+                )
+                for f in range(2):
+                    gbuf[pl.ds(4 * g + 2 * u + f, rc, stride=frames), :] = sp[f * rc : (f + 1) * rc]
+
+        def pack(j, total):
+            for ri in range(2):
+                for cc in range(cb):
+                    at = pl.multiple_of((ri * half_c + j * cb + cc) * frames, frames)
+                    tile = gbuf[pl.ds(at, frames), :].astype(jnp.bfloat16)
+                    spec[s, j, ri, :, pl.ds(cc * LANES, LANES)] = tile
+                    wide = tile.astype(jnp.float32)
+                    total = total + wide * wide
+            return total
+
+        total = lax.fori_loop(0, n, pack, jnp.zeros((frames, LANES), jnp.float32))
+        pbuf[pl.ds(s, 1), :] = jnp.sum(total, axis=0, keepdims=True)
+
+        @pl.loop(1, n)
+        def _(o):
+            peer = lax.rem(me + o, n)
+            pltpu.make_async_remote_copy(
+                src_ref=spec.at[s, peer],
+                dst_ref=recv.at[s, :, pl.ds(me * frames, frames), :],
+                send_sem=spec_send.at[s],
+                recv_sem=spec_recv.at[s],
+                device_id={"tm": peer},
+                device_id_type=MESH,
+            ).start()
+
+        pltpu.make_async_copy(
+            spec.at[s, me], recv.at[s, :, pl.ds(me * frames, frames), :], own_sem.at[s]
+        ).start()
+
+    @pl.loop(1, n)
+    def _(o):
+        peer = lax.rem(me + o, n)
+        pltpu.make_async_remote_copy(
+            src_ref=pbuf,
+            dst_ref=pall.at[me],
+            send_sem=pow_send,
+            recv_sem=pow_recv,
+            device_id={"tm": peer},
+            device_id_type=MESH,
+        ).start()
+
+    mine = pltpu.make_async_copy(pbuf, pall.at[me], pow_own)
+    mine.start()
+    mine.wait()
+    part = pall.at[pl.ds(0, n - 1)]
+    pltpu.make_async_copy(part, part, pow_recv).wait()
+    power = jnp.sum(jnp.sum(pall[...], axis=0), axis=1, keepdims=True)
+    gain = 0.378 / jnp.sqrt(power / count + 1e-06)
+    gain_buf[...] = jnp.broadcast_to(gain, gain_buf.shape)
+
+    @pl.loop(0, streams)
+    def _(s):
+        others = spec.at[s, pl.ds(0, n - 1)]
+        pltpu.make_async_copy(others, others, spec_recv.at[s]).wait()
+        pltpu.make_async_copy(
+            spec.at[s, me], recv.at[s, :, pl.ds(me * frames, frames), :], own_sem.at[s]
+        ).wait()
+        g = gain_buf[pl.ds(s, 1), :]
+        for ri in range(2):
+            flipped = lax.dot_general(
+                eye_ref[...], recv[s, ri], (((1,), (1,)), ((), ())), preferred_element_type=jnp.float32
+            )
+            scaled = jnp.clip(flipped * g, -1.0, 1.0)
+            out_ref[s, ri] = scaled.astype(jnp.bfloat16)
+
+    @pl.loop(0, streams)
+    def _(s):
+        others = spec.at[s, pl.ds(0, n - 1)]
+        pltpu.make_async_copy(others, others, spec_send.at[s]).wait()
+
+    part = pall.at[pl.ds(0, n - 1)]
+    pltpu.make_async_copy(part, part, pow_send).wait()
+
+    @pl.when(me < n - 1)
+    def _():
+        @pl.loop(0, streams)
+        def _(s):
+            halo_copy(s).wait_send()
+
+
+def on_device_kernel(samples, filter_taps):
+    n = lax.axis_size("tm")
+    streams = samples.shape[0]
+    taps, fft_len = filter_taps.shape
+    frames = samples.shape[1] // fft_len
+    rows = fft_len // LANES
+    col_len = fft_len // ROW_LEN
+    channels = fft_len // 2
+    ch = channels // n
+    stage_a, cos_t, sin_t, stage_b = kernel_tables(ROW_LEN, col_len)
+    eye = jnp.asarray(np.eye(ch), jnp.bfloat16)
+    vmem = pl.BlockSpec(memory_space=pltpu.VMEM)
+    dma = pltpu.SemaphoreType.DMA
+    return pl.pallas_call(
+        functools.partial(body, n, float(frames * n * channels)),
+        out_shape=jax.ShapeDtypeStruct((streams, 2, ch, frames * n), jnp.bfloat16),
+        in_specs=[vmem] * 7,
+        out_specs=vmem,
+        scratch_shapes=[
+            pltpu.VMEM((streams * frames * rows, LANES), jnp.float32),
+            pltpu.VMEM((taps * rows, LANES), jnp.float32),
+            pltpu.VMEM((streams, frames + taps - 1, rows, LANES), jnp.bfloat16),
+            pltpu.VMEM((frames // 2, 2 * rows, LANES), jnp.bfloat16),
+            pltpu.VMEM((col_len * frames, LANES), jnp.float32),
+            pltpu.VMEM((streams, n, 2, frames, ch), jnp.bfloat16),
+            pltpu.VMEM((streams, 2, frames * n, ch), jnp.bfloat16),
+            pltpu.VMEM((streams, LANES), jnp.float32),
+            pltpu.VMEM((n, streams, LANES), jnp.float32),
+            pltpu.VMEM((streams, frames * n), jnp.float32),
+            dma((streams,)), dma((streams,)), dma((streams,)), dma((streams,)), dma((streams,)),
+            dma, dma, dma,
+        ],
+        compiler_params=pltpu.CompilerParams(
+            collective_id=0, has_side_effects=True, vmem_limit_bytes=60 * 1024 * 1024
+        ),
+    )(samples, filter_taps, stage_a, cos_t, sin_t, stage_b, eye)
 
 
 target_level = 0.378
@@ -94,8 +361,18 @@
 
 
 def solution(mesh):
+    tm = mesh.shape["tm"]
+
+    def on_shard(samples, filter_taps):
+        fft_len = filter_taps.shape[1]
+        frames = samples.shape[1] // fft_len
+        whole_tiles = (fft_len // 2) % (tm * LANES) == 0 and (frames * tm) % LANES == 0
+        if whole_tiles and frames % 16 == 0 and fft_len == LANES * (LANES // 2):
+            return on_device_kernel(samples, filter_taps)
+        return on_device(samples, filter_taps)
+
     return jax.shard_map(
-        on_device,
+        on_shard,
         mesh=mesh,
         in_specs=(P("grp", "tm"), P()),
         out_specs=P("grp", None, "tm", None),

time: 246 us -> 83.4 us (0.34)
  the two profiles are of different devices: /device:TPU:0 before, /device:TPU:25 now
where the time goes in v1:
time: 83.4 us; the launch traced here: 83.2 us
  Pallas kernels  80.1 us (96%)
  local copies, waits for them, and re-layouts  3.1 us (4%)
    pallas_call x1, Pallas kernels, on_device_kernel(): pl.pallas_call(functools.partial(body, n, float(frames * n * channels)),...  80.1 us
    unnamed x1, local copies, waits for them, and re-layouts  3.1 us

profile of v1, /device:TPU:25, one launch (start us, length us, event | category | flops | bytes accessed | tf_op | source)
XLA Modules:
  0.0 83.2 jit_solution(15599324023778443452)
XLA Ops:
  0.0 80.1 %shard_map.73 = bf16[8,2,256,256]{3,2,1,0:T(8,128)(2,1)} custom-call(bf16[8,131072]{1,0:T(8,128)(2,1)} %x_ref.1, bf16[16,8192]{1,0:T(8,128)(2,1)} %taps_ref.1, bf16[256,128]{1,0:T(8,128)(2,1)} %constant.10.clone.ta_ref, f32[128,128]{1,0:T(8,128)} %constant.11.clone.ct_ref, f32[128,128]{1,0:T(8,128)} %constant.12.clone.st_ref, ...), custom_call_target="tpu_custom_call" | custom-call | tf_op jit(solution)/shard_map/pallas_call | solution.py:251
  80.1 3.1 %copy.9 = bf16[8,2,256,256]{3,2,1,0:T(8,128)(2,1)} copy(bf16[8,2,256,256]{3,2,1,0:T(8,128)(2,1)} %shard_map.73) | data formatting | bytes 4194304

commit v2 on v1

--- a/solution.py
+++ b/solution.py
@@ -10,6 +10,10 @@
 
 ROW_LEN = 128
 LANES = 128
+TURN = 4
+RELAY = -3
+VMEM_MIB = 60
+X_PIECES = 4
 MESH = pl.DeviceIdType.MESH
 
 
@@ -44,9 +48,10 @@
 
 
 def body(
-    n, count, x_ref, taps_ref, ta_ref, ct_ref, st_ref, tb_ref, eye_ref, out_ref,
-    xf, wf, ext, ybuf, gbuf, spec, recv, pbuf, pall, gain_buf,
+    n, count, x_hbm, taps_hbm, ta_hbm, ct_hbm, st_hbm, tb_hbm, eye_hbm, out_hbm,
+    x_ref, taps_ref, ta_ref, ct_ref, st_ref, tb_ref, eye_ref, out_ref, relay, xf, wf, ext, ybuf, gbuf, spec, recv, pbuf, pall, gain_buf,
     halo_send, halo_recv, spec_send, spec_recv, own_sem, pow_send, pow_recv, pow_own,
+    relay_send, relay_recv, x_sem, const_sem, out_sem,
 ):
     me = lax.axis_index("tm")
     streams = x_ref.shape[0]
@@ -65,23 +70,47 @@
     def _(o):
         pl.semaphore_signal(barrier, inc=1, device_id={"tm": lax.rem(me + o, n)}, device_id_type=MESH)
 
+    piece = x_ref.shape[1] // X_PIECES
+
+    def x_copy(i):
+        at = pl.ds(pl.multiple_of(i * piece, piece), piece)
+        return pltpu.make_async_copy(x_hbm.at[:, at], x_ref.at[:, at], x_sem.at[i])
+
+    @pl.loop(0, X_PIECES)
+    def _(i):
+        x_copy(i).start()
+
+    tables = [
+        (taps_hbm, taps_ref), (ta_hbm, ta_ref), (ct_hbm, ct_ref),
+        (st_hbm, st_ref), (tb_hbm, tb_ref), (eye_hbm, eye_ref),
+    ]
+    fetches = [pltpu.make_async_copy(a, b, const_sem.at[i]) for i, (a, b) in enumerate(tables)]
+    for fetch in fetches:
+        fetch.start()
+
     unroll = 16
 
-    @pl.loop(0, frames * rows // unroll)
-    def _(i):
-        for u in range(unroll):
-            q = i * unroll + u
-            v = x_ref[:, pl.ds(pl.multiple_of(q * LANES, LANES), LANES)].astype(jnp.float32)
-            xf[pl.ds(q, streams, stride=frames * rows), :] = v
-
-    @pl.loop(0, streams)
-    def _(s):
-        @pl.loop(0, frames)
-        def _(f):
-            at = pl.multiple_of((s * frames + f) * rows, rows)
-            ext[s, hist + f] = xf[pl.ds(at, rows), :].astype(jnp.bfloat16)
-
-    pl.semaphore_wait(barrier, n - 1)
+    steps = frames * rows // unroll // X_PIECES
+
+    @pl.loop(0, X_PIECES)
+    def _(c):
+        x_copy(c).wait()
+
+        @pl.loop(0, steps)
+        def _(i):
+            for u in range(unroll):
+                q = (c * steps + i) * unroll + u
+                v = x_ref[:, pl.ds(pl.multiple_of(q * LANES, LANES), LANES)].astype(jnp.float32)
+                xf[pl.ds(q, streams, stride=frames * rows), :] = v
+
+    half_s = streams // 2
+    turns = jnp.logical_and(lax.rem(me, TURN) == TURN - 1, me < n - 1)
+    relayed = jnp.logical_and(turns, jnp.logical_and(me + RELAY >= 0, me + RELAY < n))
+    source = me - RELAY
+    relays = jnp.logical_and(
+        jnp.logical_and(source >= 0, source < n - 1), lax.rem(source + n, TURN) == TURN - 1
+    )
+    direct = jnp.logical_and(me < n - 1, jnp.logical_not(relayed))
 
     def halo_copy(s):
         return pltpu.make_async_remote_copy(
@@ -93,11 +122,50 @@
             device_id_type=MESH,
         )
 
-    @pl.when(me < n - 1)
-    def _():
-        @pl.loop(0, streams)
-        def _(s):
+    def to_relay(s):
+        return pltpu.make_async_remote_copy(
+            src_ref=ext.at[s, pl.ds(frames, hist)],
+            dst_ref=relay.at[s - half_s],
+            send_sem=halo_send.at[s],
+            recv_sem=relay_recv.at[s - half_s],
+            device_id={"tm": lax.rem(me + RELAY + n, n)},
+            device_id_type=MESH,
+        )
+
+    def from_relay(s):
+        return pltpu.make_async_remote_copy(
+            src_ref=relay.at[s - half_s],
+            dst_ref=ext.at[s, pl.ds(0, hist)],
+            send_sem=relay_send.at[s - half_s],
+            recv_sem=halo_recv.at[s],
+            device_id={"tm": lax.rem(source + 1 + n, n)},
+            device_id_type=MESH,
+        )
+
+    def convert(s):
+        @pl.loop(0, frames)
+        def _(f):
+            at = pl.multiple_of((s * frames + f) * rows, rows)
+            ext[s, hist + f] = xf[pl.ds(at, rows), :].astype(jnp.bfloat16)
+
+    pl.semaphore_wait(barrier, n - 1)
+
+    @pl.loop(0, half_s)
+    def _(s):
+        convert(s)
+        convert(s + half_s)
+
+        @pl.when(me < n - 1)
+        def _():
             halo_copy(s).start()
+
+        @pl.when(direct)
+        def _():
+            halo_copy(s + half_s).start()
+
+        @pl.when(relayed)
+        def _():
+            to_relay(s + half_s).start()
 
     @pl.when(me == 0)
     def _():
@@ -105,6 +173,9 @@
         def _(s):
             ext[s, pl.ds(0, hist)] = jnp.zeros((hist, rows, LANES), jnp.bfloat16)
 
+    for fetch in fetches:
+        fetch.wait()
+
     @pl.loop(0, rows)
     def _(r):
         w = taps_ref[:, pl.ds(pl.multiple_of(r * LANES, LANES), LANES)].astype(jnp.float32)
@@ -117,6 +188,11 @@
         @pl.when(me > 0)
         def _():
             halo_copy(s).wait_recv()
+
+        @pl.when(jnp.logical_and(relays, s < half_s))
+        def _():
+            to_relay(s + half_s).wait_recv()
+            from_relay(s + half_s).start()
 
         @pl.loop(0, rows // 16)
         def _(rb):
@@ -168,9 +244,7 @@
         total = lax.fori_loop(0, n, pack, jnp.zeros((frames, LANES), jnp.float32))
         pbuf[pl.ds(s, 1), :] = jnp.sum(total, axis=0, keepdims=True)
 
-        @pl.loop(1, n)
-        def _(o):
-            peer = lax.rem(me + o, n)
+        def send(peer):
             pltpu.make_async_remote_copy(
                 src_ref=spec.at[s, peer],
                 dst_ref=recv.at[s, :, pl.ds(me * frames, frames), :],
@@ -179,6 +253,14 @@
                 device_id={"tm": peer},
                 device_id_type=MESH,
             ).start()
+
+        @pl.loop(0, n // 2)
+        def _(o):
+            send((1 - me // (n // 2)) * (n // 2) + lax.rem(me + o, n // 2))
+
+        @pl.loop(1, n // 2)
+        def _(o):
+            send(me // (n // 2) * (n // 2) + lax.rem(me + o, n // 2))
 
         pltpu.make_async_copy(
             spec.at[s, me], recv.at[s, :, pl.ds(me * frames, frames), :], own_sem.at[s]
@@ -219,6 +301,7 @@
             )
             scaled = jnp.clip(flipped * g, -1.0, 1.0)
             out_ref[s, ri] = scaled.astype(jnp.bfloat16)
+        pltpu.make_async_copy(out_ref.at[s], out_hbm.at[s], out_sem.at[s]).start()
 
     @pl.loop(0, streams)
     def _(s):
@@ -233,6 +316,16 @@
         @pl.loop(0, streams)
         def _(s):
             halo_copy(s).wait_send()
+
+    @pl.when(relays)
+    def _():
+        @pl.loop(0, half_s)
+        def _(s):
+            from_relay(s + half_s).wait_send()
+
+    @pl.loop(0, streams)
+    def _(s):
+        pltpu.make_async_copy(out_ref.at[s], out_hbm.at[s], out_sem.at[s]).wait()
 
 
 def on_device_kernel(samples, filter_taps):
@@ -246,14 +339,19 @@
     ch = channels // n
     stage_a, cos_t, sin_t, stage_b = kernel_tables(ROW_LEN, col_len)
     eye = jnp.asarray(np.eye(ch), jnp.bfloat16)
-    vmem = pl.BlockSpec(memory_space=pltpu.VMEM)
+    hbm = pl.BlockSpec(memory_space=pl.ANY)
     dma = pltpu.SemaphoreType.DMA
     return pl.pallas_call(
         functools.partial(body, n, float(frames * n * channels)),
         out_shape=jax.ShapeDtypeStruct((streams, 2, ch, frames * n), jnp.bfloat16),
-        in_specs=[vmem] * 7,
-        out_specs=vmem,
+        in_specs=[hbm] * 7,
+        out_specs=hbm,
         scratch_shapes=[
+            pltpu.VMEM(samples.shape, samples.dtype),
+            pltpu.VMEM(filter_taps.shape, filter_taps.dtype),
+            *[pltpu.VMEM(t.shape, t.dtype) for t in (stage_a, cos_t, sin_t, stage_b, eye)],
+            pltpu.VMEM((streams, 2, ch, frames * n), jnp.bfloat16),
+            pltpu.VMEM((streams // 2, taps - 1, rows, LANES), jnp.bfloat16),
             pltpu.VMEM((streams * frames * rows, LANES), jnp.float32),
             pltpu.VMEM((taps * rows, LANES), jnp.float32),
             pltpu.VMEM((streams, frames + taps - 1, rows, LANES), jnp.bfloat16),
@@ -266,9 +364,10 @@
             pltpu.VMEM((streams, frames * n), jnp.float32),
             dma((streams,)), dma((streams,)), dma((streams,)), dma((streams,)), dma((streams,)),
             dma, dma, dma,
+            dma((streams // 2,)), dma((streams // 2,)), dma((X_PIECES,)), dma((6,)), dma((streams,)),
         ],
         compiler_params=pltpu.CompilerParams(
-            collective_id=0, has_side_effects=True, vmem_limit_bytes=60 * 1024 * 1024
+            collective_id=0, has_side_effects=True, vmem_limit_bytes=VMEM_MIB * 1024 * 1024
         ),
     )(samples, filter_taps, stage_a, cos_t, sin_t, stage_b, eye)
 
@@ -367,7 +466,7 @@
         fft_len = filter_taps.shape[1]
         frames = samples.shape[1] // fft_len
         whole_tiles = (fft_len // 2) % (tm * LANES) == 0 and (frames * tm) % LANES == 0
-        if whole_tiles and frames % 16 == 0 and fft_len == LANES * (LANES // 2):
+        if whole_tiles and frames % 16 == 0 and fft_len == LANES * (LANES // 2) and tm % 2 == 0:
             return on_device_kernel(samples, filter_taps)
         return on_device(samples, filter_taps)
 

time: 83.4 us -> 77.1 us (0.924)
  the two profiles are of different devices: /device:TPU:25 before, /device:TPU:0 now
where the time goes in v2:
time: 77.1 us; the launch traced here: 76.9 us
  Pallas kernels  73.8 us (96%)
  local copies, waits for them, and re-layouts  3.1 us (4%)
    pallas_call x1, Pallas kernels, on_device_kernel(): pl.pallas_call(functools.partial(body, n, float(frames * n * channels)),...  73.8 us
    unnamed x1, local copies, waits for them, and re-layouts  3.1 us

profile of v2, /device:TPU:0, one launch (start us, length us, event | category | flops | bytes accessed | tf_op | source)
XLA Modules:
  0.0 76.9 jit_solution(5454504234716740870)
XLA Ops:
  0.0 73.8 %shard_map.73 = bf16[8,2,256,256]{3,2,1,0:T(8,128)(2,1)} custom-call(bf16[8,131072]{1,0:T(8,128)(2,1)} %x_hbm.1, bf16[16,8192]{1,0:T(8,128)(2,1)} %taps_hbm.1, bf16[256,128]{1,0:T(8,128)(2,1)} %constant.10.clone.ta_hbm, f32[128,128]{1,0:T(8,128)} %constant.11.clone.ct_hbm, f32[128,128]{1,0:T(8,128)} %constant.12.clone.st_hbm, ...), custom_call_target="tpu_custom_call" | custom-call | tf_op jit(solution)/shard_map/pallas_call | solution.py:344
  73.8 3.1 %copy.9 = bf16[8,2,256,256]{3,2,1,0:T(8,128)(2,1)} copy(bf16[8,2,256,256]{3,2,1,0:T(8,128)(2,1)} %shard_map.73) | data formatting | bytes 4194304

commit v3 on v2

--- a/solution.py
+++ b/solution.py
@@ -49,8 +49,8 @@
 
 def body(
     n, count, x_hbm, taps_hbm, ta_hbm, ct_hbm, st_hbm, tb_hbm, eye_hbm, out_hbm,
-    x_ref, taps_ref, ta_ref, ct_ref, st_ref, tb_ref, eye_ref, out_ref, relay, xf, wf, ext, ybuf, gbuf, spec, recv, pbuf, pall, gain_buf,
-    halo_send, halo_recv, spec_send, spec_recv, own_sem, pow_send, pow_recv, pow_own,
+    x_ref, taps_ref, ta_ref, ct_ref, st_ref, tb_ref, eye_ref, out_ref, relay, xf, wf, ext, ybuf, gbuf, spec, recv, pall,
+    halo_send, halo_recv, spec_send, spec_recv, own_sem, pow_send, pow_recv,
     relay_send, relay_recv, x_sem, const_sem, out_sem,
 ):
     me = lax.axis_index("tm")
@@ -242,9 +242,17 @@
             return total
 
         total = lax.fori_loop(0, n, pack, jnp.zeros((frames, LANES), jnp.float32))
-        pbuf[pl.ds(s, 1), :] = jnp.sum(total, axis=0, keepdims=True)
+        pall[s, me] = jnp.sum(total, axis=0, keepdims=True)
 
         def send(peer):
+            pltpu.make_async_remote_copy(
+                src_ref=pall.at[s, me],
+                dst_ref=pall.at[s, me],
+                send_sem=pow_send.at[s],
+                recv_sem=pow_recv.at[s],
+                device_id={"tm": peer},
+                device_id_type=MESH,
+            ).start()
             pltpu.make_async_remote_copy(
                 src_ref=spec.at[s, peer],
                 dst_ref=recv.at[s, :, pl.ds(me * frames, frames), :],
@@ -266,27 +274,6 @@
             spec.at[s, me], recv.at[s, :, pl.ds(me * frames, frames), :], own_sem.at[s]
         ).start()
 
-    @pl.loop(1, n)
-    def _(o):
-        peer = lax.rem(me + o, n)
-        pltpu.make_async_remote_copy(
-            src_ref=pbuf,
-            dst_ref=pall.at[me],
-            send_sem=pow_send,
-            recv_sem=pow_recv,
-            device_id={"tm": peer},
-            device_id_type=MESH,
-        ).start()
-
-    mine = pltpu.make_async_copy(pbuf, pall.at[me], pow_own)
-    mine.start()
-    mine.wait()
-    part = pall.at[pl.ds(0, n - 1)]
-    pltpu.make_async_copy(part, part, pow_recv).wait()
-    power = jnp.sum(jnp.sum(pall[...], axis=0), axis=1, keepdims=True)
-    gain = 0.378 / jnp.sqrt(power / count + 1e-06)
-    gain_buf[...] = jnp.broadcast_to(gain, gain_buf.shape)
-
     @pl.loop(0, streams)
     def _(s):
         others = spec.at[s, pl.ds(0, n - 1)]
@@ -294,7 +281,10 @@
         pltpu.make_async_copy(
             spec.at[s, me], recv.at[s, :, pl.ds(me * frames, frames), :], own_sem.at[s]
         ).wait()
-        g = gain_buf[pl.ds(s, 1), :]
+        part = pall.at[s, pl.ds(0, n - 1)]
+        pltpu.make_async_copy(part, part, pow_recv.at[s]).wait()
+        power = jnp.sum(jnp.sum(pall[s], axis=0), axis=1, keepdims=True)
+        g = 0.378 / jnp.sqrt(power / count + 1e-06)
         for ri in range(2):
             flipped = lax.dot_general(
                 eye_ref[...], recv[s, ri], (((1,), (1,)), ((), ())), preferred_element_type=jnp.float32
@@ -307,9 +297,8 @@
     def _(s):
         others = spec.at[s, pl.ds(0, n - 1)]
         pltpu.make_async_copy(others, others, spec_send.at[s]).wait()
-
-    part = pall.at[pl.ds(0, n - 1)]
-    pltpu.make_async_copy(part, part, pow_send).wait()
+        part = pall.at[s, pl.ds(0, n - 1)]
+        pltpu.make_async_copy(part, part, pow_send.at[s]).wait()
 
     @pl.when(me < n - 1)
     def _():
@@ -359,11 +348,9 @@
             pltpu.VMEM((col_len * frames, LANES), jnp.float32),
             pltpu.VMEM((streams, n, 2, frames, ch), jnp.bfloat16),
             pltpu.VMEM((streams, 2, frames * n, ch), jnp.bfloat16),
-            pltpu.VMEM((streams, LANES), jnp.float32),
-            pltpu.VMEM((n, streams, LANES), jnp.float32),
-            pltpu.VMEM((streams, frames * n), jnp.float32),
+            pltpu.VMEM((streams, n, 1, LANES), jnp.float32),
             dma((streams,)), dma((streams,)), dma((streams,)), dma((streams,)), dma((streams,)),
-            dma, dma, dma,
+            dma((streams,)), dma((streams,)),
             dma((streams // 2,)), dma((streams // 2,)), dma((X_PIECES,)), dma((6,)), dma((streams,)),
         ],
         compiler_params=pltpu.CompilerParams(

time: 77.1 us -> 74 us (0.960)
  Pallas kernels: 73.8 us -> 70.7 us
    pallas_call x1, Pallas kernels: 73.8 us -> 70.7 us  [on_device_kernel(): pl.pallas_call(functools.partial(body, n, float(frames * n * channels)),...]
where the time goes in v3:
time: 74 us; the launch traced here: 73.8 us
  Pallas kernels  70.7 us (96%)
  local copies, waits for them, and re-layouts  3.1 us (4%)
    pallas_call x1, Pallas kernels, on_device_kernel(): pl.pallas_call(functools.partial(body, n, float(frames * n * channels)),...  70.7 us
    unnamed x1, local copies, waits for them, and re-layouts  3.1 us

profile of v3, /device:TPU:0, one launch (start us, length us, event | category | flops | bytes accessed | tf_op | source)
XLA Modules:
  0.0 73.8 jit_solution(6369098988387522937)
XLA Ops:
  0.0 70.7 %shard_map.73 = bf16[8,2,256,256]{3,2,1,0:T(8,128)(2,1)} custom-call(bf16[8,131072]{1,0:T(8,128)(2,1)} %x_hbm.1, bf16[16,8192]{1,0:T(8,128)(2,1)} %taps_hbm.1, bf16[256,128]{1,0:T(8,128)(2,1)} %constant.10.clone.ta_hbm, f32[128,128]{1,0:T(8,128)} %constant.11.clone.ct_hbm, f32[128,128]{1,0:T(8,128)} %constant.12.clone.st_hbm, ...), custom_call_target="tpu_custom_call" | custom-call | tf_op jit(solution)/shard_map/pallas_call | solution.py:333
  70.7 3.1 %copy.9 = bf16[8,2,256,256]{3,2,1,0:T(8,128)(2,1)} copy(bf16[8,2,256,256]{3,2,1,0:T(8,128)(2,1)} %shard_map.73) | data formatting | bytes 4194304
